TPU v7x, 32 devices: a 4x4x1 block of a 4x4x8 slice. The times are simulated.
32 devices in a mesh: rep: 2 (over z, core), dp: 16 (over x, y).
Axes of the slice: x: 4, y: 4, z: 1, core: 2. Of those that a mesh axis runs over, the one named last changes fastest.
The devices are a block of a 4x4x8 slice.
Arguments:
- a: bfloat16 [32, 4, 4096, 896], P(('rep', 'dp')), parts along dimension 0
- g: bfloat16 [32, 4, 4096, 2304], P(('rep', 'dp')), parts along dimension 0
Outputs:
- output: bfloat16 [8, 896, 2304], P('rep'), parts along dimension 0
There are 2 independent parts. A program takes and returns all parts, laid end to end along the dimension named above; each array names one.
All inputs are finite; a program needn't handle non-finite values.
Results may differ from a plain program's by a relative error of at most 0.012.
Values are sent between devices in bfloat16 or wider.
A program may use at most 768 MiB of HBM per device.

v0:
```python
import jax
import jax.numpy as jnp


def solution(mesh):
    groups = mesh.shape["rep"]

    def step(a, g):
        a, g = (t.reshape(groups, -1, *t.shape[1:]) for t in (a, g))
        sums = jnp.einsum("rsntd,rsntf->rndf", a, g, preferred_element_type=jnp.float32)
        return sums.astype(jnp.bfloat16).reshape(-1, *sums.shape[2:])

    return step
```

profile of v0, /device:TPU:97, one launch (start us, length us, event | category | flops | bytes accessed | tf_op | source)
XLA Modules:
  0.0 787.9 jit_solution(4298790847336297651)
XLA Ops:
  0.0 78.6 %fusion.3 = f32[1,4,896,2304]{3,2,1,0:T(8,128)} fusion(bf16[1,4,4096,2304]{3,2,1,0:T(8,128)(2,1)} %param.1, bf16[1,4,4096,896]{3,2,1,0:T(8,128)(2,1)} %param), kind=kOutput, calls=%fused_computation.3 | convolution fusion | flops 67645734912 | bytes 137887744 | tf_op jit(solution)/rsntd,rsntf->rndf/dot_general | solution.py:10
  78.6 709.3 %all-reduce.2 = bf16[1,4,896,2304]{3,2,1,0:T(8,128)(2,1)} all-reduce(f32[1,4,896,2304]{3,2,1,0:T(8,128)} %fusion.3), channel_id=1, replica_groups=[2,16]<=[32], use_global_device_ids=true, to_apply=%add.clone | all-reduce | flops 8257536 | bytes 49545216 | tf_op jit(solution)/rsntd,rsntf->rndf/dot_general | solution.py:10
where the time goes:
time: 788 us
  blocking collectives  709 us (90%)
  matrix products  78.6 us (10%)
    dot_general x1, blocking collectives, step(): jnp.einsum('rsntd,rsntf->rndf', a, g, preferred_element_type=jnp.float32)  709 us
    dot_general x1, matrix products, step(): jnp.einsum('rsntd,rsntf->rndf', a, g, preferred_element_type=jnp.float32)  78.6 us

commit v1 on v0

v1 whole, which is shorter than its diff:
```python
import functools
import math

import jax
import jax.numpy as jnp
from jax import lax
from jax.experimental import pallas as pl
from jax.experimental.pallas import tpu as pltpu
from jax.sharding import PartitionSpec as P

MESH = pl.DeviceIdType.MESH
F32, BF16 = jnp.float32, jnp.bfloat16

WIDTH = 256
LAG = 2
STAGES = 10
LANDING = 4 * LAG + 4
LEAVING = 2 * LAG + 2
TURN = 512


def kernel(side, a_hbm, g_hbm, out, raw, turned, g_buf, acc, half, far_out, near_out, far_in, near_in, raw_sem, g_sem, send, recv):
    matrices, tokens, d = a_hbm.shape
    per_matrix = g_hbm.shape[2] // WIDTH
    pieces = matrices * per_matrix
    quarter = d // side
    part = quarter // side
    rep, me = lax.axis_index("rep"), lax.axis_index("dp")

    def step_from(axis, delta):
        stride = side * (1 - axis) + axis
        at = (me // stride) % side
        return me + ((at + delta + side) % side - at) * stride

    barrier = pltpu.get_barrier_semaphore()
    for axis in (0, 1):
        for delta in (1, -1):
            pl.semaphore_signal(barrier, inc=1, device_id=(rep, step_from(axis, delta)), device_id_type=MESH)

    def load_a(n):
        return pltpu.make_async_copy(a_hbm.at[n], raw, raw_sem)

    def load_g(k):
        columns = pl.ds(pl.multiple_of((k % per_matrix) * WIDTH, WIDTH), WIDTH)
        return pltpu.make_async_copy(g_hbm.at[k // per_matrix, :, columns], g_buf.at[k % 2], g_sem.at[k % 2])

    load_a(0).start()
    load_g(0).start()
    pl.semaphore_wait(barrier, 4)

    class Piece:
        def __init__(self, k):
            self.k = k
            self.axis = k % 2
            self.way = 1 - 2 * ((k // 2 + rep) % 2)
            stride = side * (1 - self.axis) + self.axis
            self.at = ((me // stride) % side, (me // (side + 1 - stride)) % side)
            self.land, self.leave = k % LANDING, k % LEAVING

        def rows(self, phase, delta):
            size = (quarter, part)[phase]
            owner = (self.at[phase] + delta * self.way + 2 * side) % side
            return pl.ds(pl.multiple_of(owner * size, size), size)

        def own(self, delta):
            owner = (self.at[1] + delta * self.way + 2 * side) % side
            return pl.ds(pl.multiple_of(self.at[0] * quarter + owner * part, part), part)

        def copy(self, src, dst, phase, message):
            second = 1 if phase in (1, 2) else 0
            axis = self.axis * (1 - second) + (1 - self.axis) * second
            delta = self.way if message != 1 else -self.way
            return pltpu.make_async_remote_copy(
                src_ref=src,
                dst_ref=dst,
                send_sem=send.at[phase, message, self.leave],
                recv_sem=recv.at[phase, message, self.land],
                device_id=(rep, step_from(axis, delta)),
                device_id_type=MESH,
            )

        def reduce_copy(self, phase, message):
            leaving, landing = ((far_out, far_in), (near_out, near_in))[phase]
            return self.copy(leaving.at[self.leave, message], landing.at[self.land, message], phase, message)

        def landed(self, phase, message):
            return ((far_in, near_in)[phase])[self.land, message].astype(F32)

        def gather_copy(self, phase, message, rows):
            where = out.at[self.k, rows, :]
            return self.copy(where, where, phase, message)

        def gather_rows(self, phase, message):
            delta = 0 if message != 2 else -1
            return self.own(delta) if phase == 2 else self.rows(0, delta)

        def gather(self, phase, message):
            return self.gather_copy(phase, message, self.gather_rows(phase, message))

    def stage0(k):
        n, j = k // per_matrix, k % per_matrix

        @pl.when(j == 0)
        def _():
            load_a(n).wait()

            @pl.loop(0, tokens // TURN)
            def _(t):
                at = pl.multiple_of(t * TURN, TURN)
                turned[:, pl.ds(at, TURN)] = raw[pl.ds(at, TURN), :].T

            @pl.when(n + 1 < matrices)
            def _():
                load_a(n + 1).start()

        load_g(k).wait()

        @pl.when(k + 1 < pieces)
        def _():
            load_g(k + 1).start()

        p = Piece(k)
        slot = k % LEAVING

        @pl.loop(0, side)
        def _(r):
            rows = pl.ds(pl.multiple_of(r * quarter, quarter), quarter)
            acc[slot, rows, :] = jnp.dot(turned[rows, :], g_buf[k % 2], preferred_element_type=F32)

        far_out[p.leave, 0] = acc[slot, p.rows(0, 2), :].astype(BF16)
        far_out[p.leave, 1] = acc[slot, p.rows(0, -1), :].astype(BF16)
        p.reduce_copy(0, 0).start()
        p.reduce_copy(0, 1).start()

    def stage1(k):
        p = Piece(k)
        p.reduce_copy(0, 0).wait_recv()
        far_out[p.leave, 2] = (acc[k % LEAVING, p.rows(0, 1), :] + p.landed(0, 0)).astype(BF16)
        p.reduce_copy(0, 2).start()

    def stage2(k):
        p = Piece(k)
        p.reduce_copy(0, 1).wait_recv()
        p.reduce_copy(0, 2).wait_recv()
        slot = k % LEAVING
        half[slot] = acc[slot, p.rows(0, 0), :] + p.landed(0, 1) + p.landed(0, 2)
        near_out[p.leave, 0] = half[slot, p.rows(1, 2), :].astype(BF16)
        near_out[p.leave, 1] = half[slot, p.rows(1, -1), :].astype(BF16)
        p.reduce_copy(0, 0).wait_send()
        p.reduce_copy(0, 1).wait_send()
        p.reduce_copy(1, 0).start()
        p.reduce_copy(1, 1).start()

    def stage3(k):
        p = Piece(k)
        p.reduce_copy(1, 0).wait_recv()
        near_out[p.leave, 2] = (half[k % LEAVING, p.rows(1, 1), :] + p.landed(1, 0)).astype(BF16)
        p.reduce_copy(0, 2).wait_send()
        p.reduce_copy(1, 2).start()

    def stage4(k):
        p = Piece(k)
        p.reduce_copy(1, 1).wait_recv()
        p.reduce_copy(1, 2).wait_recv()
        out[k, p.own(0), :] = (half[k % LEAVING, p.rows(1, 0), :] + p.landed(1, 1) + p.landed(1, 2)).astype(BF16)
        p.reduce_copy(1, 0).wait_send()
        p.reduce_copy(1, 1).wait_send()
        p.gather(2, 0).start()
        p.gather(2, 1).start()

    def stage5(k):
        p = Piece(k)
        p.gather(2, 0).wait_recv()
        p.reduce_copy(1, 2).wait_send()
        p.gather(2, 2).start()

    def stage6(k):
        p = Piece(k)
        p.gather(2, 1).wait_recv()
        p.gather(2, 2).wait_recv()
        p.gather(2, 0).wait_send()
        p.gather(2, 1).wait_send()
        p.gather(3, 0).start()
        p.gather(3, 1).start()

    def stage7(k):
        p = Piece(k)
        p.gather(3, 0).wait_recv()
        p.gather(2, 2).wait_send()
        p.gather(3, 2).start()

    def stage8(k):
        p = Piece(k)
        p.gather(3, 1).wait_recv()
        p.gather(3, 2).wait_recv()
        p.gather(3, 0).wait_send()
        p.gather(3, 1).wait_send()

    def stage9(k):
        Piece(k).gather(3, 2).wait_send()

    stages = (stage0, stage1, stage2, stage3, stage4, stage5, stage6, stage7, stage8, stage9)
    assert len(stages) == STAGES

    @pl.loop(0, pieces + (STAGES - 1) * LAG)
    def _(i):
        for s in reversed(range(STAGES)):
            k = i - s * LAG

            @pl.when((k >= 0) & (k < pieces))
            def _(s=s, k=k):
                stages[s](k)


def place(held, out, sem):
    matrices, per_matrix = out.shape[0], out.shape[2] // WIDTH

    def move(k):
        columns = pl.ds(pl.multiple_of((k % per_matrix) * WIDTH, WIDTH), WIDTH)
        return pltpu.make_async_copy(held.at[k], out.at[k // per_matrix, :, columns], sem.at[k])

    for k in range(matrices * per_matrix):
        move(k).start()
    for k in range(matrices * per_matrix):
        move(k).wait()


def solution(mesh):
    side = math.isqrt(mesh.shape["dp"])

    def local(a, g):
        a, g = a[0], g[0]
        matrices, tokens, d = a.shape
        ff = g.shape[2]
        pieces = matrices * (ff // WIDTH)
        quarter = d // side
        part = quarter // side
        held = pl.pallas_call(
            functools.partial(kernel, side),
            out_shape=pltpu.VMEM((pieces, d, WIDTH), BF16),
            in_specs=[pl.BlockSpec(memory_space=pltpu.HBM)] * 2,
            out_specs=pl.BlockSpec(memory_space=pltpu.VMEM),
            scratch_shapes=[
                pltpu.VMEM((tokens, d), BF16),
                pltpu.VMEM((d, tokens), BF16),
                pltpu.VMEM((2, tokens, WIDTH), BF16),
                pltpu.VMEM((LEAVING, d, WIDTH), F32),
                pltpu.VMEM((LEAVING, quarter, WIDTH), F32),
                pltpu.VMEM((LEAVING, 3, quarter, WIDTH), BF16),
                pltpu.VMEM((LEAVING, 3, part, WIDTH), BF16),
                pltpu.VMEM((LANDING, 3, quarter, WIDTH), BF16),
                pltpu.VMEM((LANDING, 3, part, WIDTH), BF16),
                pltpu.SemaphoreType.DMA,
                pltpu.SemaphoreType.DMA((2,)),
                pltpu.SemaphoreType.DMA((4, 3, LEAVING)),
                pltpu.SemaphoreType.DMA((4, 3, LANDING)),
            ],
            compiler_params=pltpu.CompilerParams(
                collective_id=0, has_side_effects=True, vmem_limit_bytes=44 * 2**20
            ),
            cost_estimate=pl.CostEstimate(
                flops=2 * matrices * tokens * d * ff,
                bytes_accessed=2 * matrices * tokens * (d + ff),
                transcendentals=0,
            ),
            name="sum_over_group",
        )(a, g)
        return pl.pallas_call(
            place,
            out_shape=jax.ShapeDtypeStruct((matrices, d, ff), BF16),
            in_specs=[pl.BlockSpec(memory_space=pltpu.VMEM)],
            out_specs=pl.BlockSpec(memory_space=pltpu.HBM),
            scratch_shapes=[pltpu.SemaphoreType.DMA((pieces,))],
            compiler_params=pltpu.CompilerParams(vmem_limit_bytes=2**20),
            name="place",
        )(held)

    return jax.shard_map(
        local,
        mesh=mesh,
        in_specs=(P(("rep", "dp")), P(("rep", "dp"))),
        out_specs=P("rep"),
        check_vma=False,
    )
```

time: 788 us -> 213 us (0.27)
  blocking collectives: 709 us -> 0 us
  Pallas kernels: 0 us -> 212 us
  matrix products: 78.6 us -> 0 us
    dot_general x1 -> x0, blocking collectives: 709 us -> none  [step(): jnp.einsum('rsntd,rsntf->rndf', a, g, preferred_element_type=jnp.float32)]
    pallas_call x0 -> x2, Pallas kernels: none -> 212 us  [the longest x1 206 us: local(): pl.pallas_call(functools.partial(kernel, side), out_shape=pltpu.VMEM((pie...]
    dot_general x1 -> x0, matrix products: 78.6 us -> none  [step(): jnp.einsum('rsntd,rsntf->rndf', a, g, preferred_element_type=jnp.float32)]
where the time goes in v1:
time: 213 us; the launch traced here: 212 us
  Pallas kernels  212 us (100%)
    pallas_call x1, Pallas kernels, local(): pl.pallas_call(functools.partial(kernel, side), out_shape=pltpu.VMEM((pie...  206 us
    pallas_call x1, Pallas kernels, local(): pl.pallas_call(place, out_shape=jax.ShapeDtypeStruct((matrices, d, ff), B...  6.04 us

profile of v1, /device:TPU:97, one launch (start us, length us, event | category | flops | bytes accessed | tf_op | source)
XLA Modules:
  0.0 212.1 jit_solution(17412491977037407070)
XLA Ops:
  0.0 206.1 %sum_over_group.1.held = bf16[36,896,256]{2,1,0:T(8,128)(2,1)S(1)} custom-call(bf16[4,4096,896]{2,1,0:T(8,128)(2,1)} %bitcast.2, bf16[4,4096,2304]{2,1,0:T(8,128)(2,1)} %bitcast.1.g_hbm), custom_call_target="tpu_custom_call" | custom-call | flops 67645734912 | bytes 104857600 | tf_op jit(solution)/shard_map/sum_over_group/pallas_call | solution.py:238
  206.1 6.0 %place.1 = bf16[4,896,2304]{2,1,0:T(8,128)(2,1)} custom-call(bf16[36,896,256]{2,1,0:T(8,128)(2,1)S(1)} %sum_over_group.1.held), custom_call_target="tpu_custom_call" | custom-call | tf_op jit(solution)/shard_map/place/pallas_call | solution.py:268

commit v2 on v1

--- a/solution.py
+++ b/solution.py
@@ -12,14 +12,15 @@
 F32, BF16 = jnp.float32, jnp.bfloat16
 
 WIDTH = 256
-LAG = 2
-STAGES = 10
-LANDING = 4 * LAG + 4
-LEAVING = 2 * LAG + 2
+LAGS = (0, 3, 6, 9, 12, 15, 18, 21, 24, 27)
+LEAVING = max(later - sooner for sooner, later in zip(LAGS, LAGS[2:]))
+LANDING = 2 * LEAVING + 4
 TURN = 512
-
-
-def kernel(side, a_hbm, g_hbm, out, raw, turned, g_buf, acc, half, far_out, near_out, far_in, near_in, raw_sem, g_sem, send, recv):
+RAW = 4
+AHEAD = 2
+
+
+def kernel(side, a_hbm, g_hbm, out, raw, turned_even, turned_odd, g_buf, acc, half, far_out, near_out, far_in, near_in, raw_sem, g_sem, send, recv):
     matrices, tokens, d = a_hbm.shape
     per_matrix = g_hbm.shape[2] // WIDTH
     pieces = matrices * per_matrix
@@ -37,15 +38,36 @@
         for delta in (1, -1):
             pl.semaphore_signal(barrier, inc=1, device_id=(rep, step_from(axis, delta)), device_id_type=MESH)
 
-    def load_a(n):
-        return pltpu.make_async_copy(a_hbm.at[n], raw, raw_sem)
+    blocks = tokens // TURN
+
+    def load_a(q):
+        at = pl.ds(pl.multiple_of((q % blocks) * TURN, TURN), TURN)
+        return pltpu.make_async_copy(a_hbm.at[q // blocks, at, :], raw.at[q % RAW], raw_sem.at[q % RAW])
 
     def load_g(k):
         columns = pl.ds(pl.multiple_of((k % per_matrix) * WIDTH, WIDTH), WIDTH)
-        return pltpu.make_async_copy(g_hbm.at[k // per_matrix, :, columns], g_buf.at[k % 2], g_sem.at[k % 2])
-
-    load_a(0).start()
-    load_g(0).start()
+        slot = k % (AHEAD + 1)
+        return pltpu.make_async_copy(g_hbm.at[k // per_matrix, :, columns], g_buf.at[slot], g_sem.at[slot])
+
+    def turn(q, turned):
+        at = pl.ds(pl.multiple_of((q % blocks) * TURN, TURN), TURN)
+        turned[:, at] = raw[q % RAW].T
+
+    for q in range(RAW):
+        load_a(q).start()
+    for k in range(AHEAD):
+        load_g(k).start()
+
+    @pl.loop(0, blocks)
+    def _(q):
+        load_a(q).wait()
+
+        @pl.when(q > 0)
+        def _():
+            load_a(q - 1 + RAW).start()
+
+        turn(q, turned_even)
+
     pl.semaphore_wait(barrier, 4)
 
     class Piece:
@@ -99,33 +121,37 @@
 
     def stage0(k):
         n, j = k // per_matrix, k % per_matrix
-
-        @pl.when(j == 0)
-        def _():
-            load_a(n).wait()
-
-            @pl.loop(0, tokens // TURN)
-            def _(t):
-                at = pl.multiple_of(t * TURN, TURN)
-                turned[:, pl.ds(at, TURN)] = raw[pl.ds(at, TURN), :].T
-
-            @pl.when(n + 1 < matrices)
+        fresh = j < blocks
+        q = (n + 1) * blocks + jnp.minimum(j, blocks - 1)
+
+        @pl.when(fresh & (n + 1 < matrices))
+        def _():
+            load_a(q).wait()
+
+            @pl.when(q - 1 + RAW < matrices * blocks)
             def _():
-                load_a(n + 1).start()
+                load_a(q - 1 + RAW).start()
 
         load_g(k).wait()
 
-        @pl.when(k + 1 < pieces)
-        def _():
-            load_g(k + 1).start()
+        @pl.when(k + AHEAD < pieces)
+        def _():
+            load_g(k + AHEAD).start()
 
         p = Piece(k)
         slot = k % LEAVING
 
-        @pl.loop(0, side)
-        def _(r):
-            rows = pl.ds(pl.multiple_of(r * quarter, quarter), quarter)
-            acc[slot, rows, :] = jnp.dot(turned[rows, :], g_buf[k % 2], preferred_element_type=F32)
+        def compute(turned, turned_next):
+            turn(q, turned_next)
+            acc[slot] = jnp.dot(turned[...], g_buf[k % (AHEAD + 1)], preferred_element_type=F32)
+
+        @pl.when(n % 2 == 0)
+        def _():
+            compute(turned_even, turned_odd)
+
+        @pl.when(n % 2 == 1)
+        def _():
+            compute(turned_odd, turned_even)
 
         far_out[p.leave, 0] = acc[slot, p.rows(0, 2), :].astype(BF16)
         far_out[p.leave, 1] = acc[slot, p.rows(0, -1), :].astype(BF16)
@@ -200,12 +226,11 @@
         Piece(k).gather(3, 2).wait_send()
 
     stages = (stage0, stage1, stage2, stage3, stage4, stage5, stage6, stage7, stage8, stage9)
-    assert len(stages) == STAGES
-
-    @pl.loop(0, pieces + (STAGES - 1) * LAG)
+
+    @pl.loop(0, pieces + LAGS[-1])
     def _(i):
-        for s in reversed(range(STAGES)):
-            k = i - s * LAG
+        for s in reversed(range(len(stages))):
+            k = i - LAGS[s]
 
             @pl.when((k >= 0) & (k < pieces))
             def _(s=s, k=k):
@@ -241,22 +266,23 @@
             in_specs=[pl.BlockSpec(memory_space=pltpu.HBM)] * 2,
             out_specs=pl.BlockSpec(memory_space=pltpu.VMEM),
             scratch_shapes=[
-                pltpu.VMEM((tokens, d), BF16),
+                pltpu.VMEM((RAW, TURN, d), BF16),
                 pltpu.VMEM((d, tokens), BF16),
-                pltpu.VMEM((2, tokens, WIDTH), BF16),
+                pltpu.VMEM((d, tokens), BF16),
+                pltpu.VMEM((AHEAD + 1, tokens, WIDTH), BF16),
                 pltpu.VMEM((LEAVING, d, WIDTH), F32),
                 pltpu.VMEM((LEAVING, quarter, WIDTH), F32),
                 pltpu.VMEM((LEAVING, 3, quarter, WIDTH), BF16),
                 pltpu.VMEM((LEAVING, 3, part, WIDTH), BF16),
                 pltpu.VMEM((LANDING, 3, quarter, WIDTH), BF16),
                 pltpu.VMEM((LANDING, 3, part, WIDTH), BF16),
-                pltpu.SemaphoreType.DMA,
-                pltpu.SemaphoreType.DMA((2,)),
+                pltpu.SemaphoreType.DMA((RAW,)),
+                pltpu.SemaphoreType.DMA((AHEAD + 1,)),
                 pltpu.SemaphoreType.DMA((4, 3, LEAVING)),
                 pltpu.SemaphoreType.DMA((4, 3, LANDING)),
             ],
             compiler_params=pltpu.CompilerParams(
-                collective_id=0, has_side_effects=True, vmem_limit_bytes=44 * 2**20
+                collective_id=0, has_side_effects=True, vmem_limit_bytes=47 * 2**20
             ),
             cost_estimate=pl.CostEstimate(
                 flops=2 * matrices * tokens * d * ff,

time: 213 us -> 199 us (0.934)
  Pallas kernels: 212 us -> 199 us
    pallas_call x1, Pallas kernels: 206 us -> 193 us  [local(): pl.pallas_call(functools.partial(kernel, side), out_shape=pltpu.VMEM((pie...]
where the time goes in v2:
time: 199 us
  Pallas kernels  199 us (100%)
    pallas_call x1, Pallas kernels, local(): pl.pallas_call(functools.partial(kernel, side), out_shape=pltpu.VMEM((pie...  193 us
    pallas_call x1, Pallas kernels, local(): pl.pallas_call(place, out_shape=jax.ShapeDtypeStruct((matrices, d, ff), B...  6.04 us

profile of v2, /device:TPU:97, one launch (start us, length us, event | category | flops | bytes accessed | tf_op | source)
XLA Modules:
  0.0 199.0 jit_solution(9081007932547415338)
XLA Ops:
  0.0 192.9 %sum_over_group.1.held = bf16[36,896,256]{2,1,0:T(8,128)(2,1)S(1)} custom-call(bf16[4,4096,896]{2,1,0:T(8,128)(2,1)} %bitcast.2, bf16[4,4096,2304]{2,1,0:T(8,128)(2,1)} %bitcast.1.g_hbm), custom_call_target="tpu_custom_call" | custom-call | flops 67645734912 | bytes 104857600 | tf_op jit(solution)/shard_map/sum_over_group/pallas_call | solution.py:263
  192.9 6.0 %place.1 = bf16[4,896,2304]{2,1,0:T(8,128)(2,1)} custom-call(bf16[36,896,256]{2,1,0:T(8,128)(2,1)S(1)} %sum_over_group.1.held), custom_call_target="tpu_custom_call" | custom-call | tf_op jit(solution)/shard_map/place/pallas_call | solution.py:294

commit v3 on v2

--- a/solution.py
+++ b/solution.py
@@ -12,9 +12,13 @@
 F32, BF16 = jnp.float32, jnp.bfloat16
 
 WIDTH = 256
-LAGS = (0, 3, 6, 9, 12, 15, 18, 21, 24, 27)
-LEAVING = max(later - sooner for sooner, later in zip(LAGS, LAGS[2:]))
+LAGS = (0, 3, 5, 8, 10, 12, 15, 18, 20, 22)
+ORDER = (0, 1, 2, 3, 4, 5, 6, 7, 8, 9)
+APART = tuple(later - sooner for sooner, later in zip(LAGS, LAGS[2:]))
+LEAVING = max(APART) + 1
 LANDING = 2 * LEAVING + 4
+KEPT = max(APART[:4]) + 1
+HELD = 2 * KEPT + 4
 TURN = 512
 RAW = 4
 AHEAD = 2
@@ -78,6 +82,7 @@
             stride = side * (1 - self.axis) + self.axis
             self.at = ((me // stride) % side, (me // (side + 1 - stride)) % side)
             self.land, self.leave = k % LANDING, k % LEAVING
+            self.kept, self.held = k % KEPT, k % HELD
 
         def rows(self, phase, delta):
             size = (quarter, part)[phase]
@@ -103,10 +108,10 @@
 
         def reduce_copy(self, phase, message):
             leaving, landing = ((far_out, far_in), (near_out, near_in))[phase]
-            return self.copy(leaving.at[self.leave, message], landing.at[self.land, message], phase, message)
+            return self.copy(leaving.at[self.kept, message], landing.at[self.held, message], phase, message)
 
         def landed(self, phase, message):
-            return ((far_in, near_in)[phase])[self.land, message].astype(F32)
+            return ((far_in, near_in)[phase])[self.held, message].astype(F32)
 
         def gather_copy(self, phase, message, rows):
             where = out.at[self.k, rows, :]
@@ -139,7 +144,7 @@
             load_g(k + AHEAD).start()
 
         p = Piece(k)
-        slot = k % LEAVING
+        slot = k % KEPT
 
         def compute(turned, turned_next):
             turn(q, turned_next)
@@ -153,25 +158,25 @@
         def _():
             compute(turned_odd, turned_even)
 
-        far_out[p.leave, 0] = acc[slot, p.rows(0, 2), :].astype(BF16)
-        far_out[p.leave, 1] = acc[slot, p.rows(0, -1), :].astype(BF16)
+        far_out[p.kept, 0] = acc[slot, p.rows(0, 2), :].astype(BF16)
+        far_out[p.kept, 1] = acc[slot, p.rows(0, -1), :].astype(BF16)
         p.reduce_copy(0, 0).start()
         p.reduce_copy(0, 1).start()
 
     def stage1(k):
         p = Piece(k)
         p.reduce_copy(0, 0).wait_recv()
-        far_out[p.leave, 2] = (acc[k % LEAVING, p.rows(0, 1), :] + p.landed(0, 0)).astype(BF16)
+        far_out[p.kept, 2] = (acc[k % KEPT, p.rows(0, 1), :] + p.landed(0, 0)).astype(BF16)
         p.reduce_copy(0, 2).start()
 
     def stage2(k):
         p = Piece(k)
         p.reduce_copy(0, 1).wait_recv()
         p.reduce_copy(0, 2).wait_recv()
-        slot = k % LEAVING
+        slot = k % KEPT
         half[slot] = acc[slot, p.rows(0, 0), :] + p.landed(0, 1) + p.landed(0, 2)
-        near_out[p.leave, 0] = half[slot, p.rows(1, 2), :].astype(BF16)
-        near_out[p.leave, 1] = half[slot, p.rows(1, -1), :].astype(BF16)
+        near_out[p.kept, 0] = half[slot, p.rows(1, 2), :].astype(BF16)
+        near_out[p.kept, 1] = half[slot, p.rows(1, -1), :].astype(BF16)
         p.reduce_copy(0, 0).wait_send()
         p.reduce_copy(0, 1).wait_send()
         p.reduce_copy(1, 0).start()
@@ -180,7 +185,7 @@
     def stage3(k):
         p = Piece(k)
         p.reduce_copy(1, 0).wait_recv()
-        near_out[p.leave, 2] = (half[k % LEAVING, p.rows(1, 1), :] + p.landed(1, 0)).astype(BF16)
+        near_out[p.kept, 2] = (half[k % KEPT, p.rows(1, 1), :] + p.landed(1, 0)).astype(BF16)
         p.reduce_copy(0, 2).wait_send()
         p.reduce_copy(1, 2).start()
 
@@ -188,7 +193,7 @@
         p = Piece(k)
         p.reduce_copy(1, 1).wait_recv()
         p.reduce_copy(1, 2).wait_recv()
-        out[k, p.own(0), :] = (half[k % LEAVING, p.rows(1, 0), :] + p.landed(1, 1) + p.landed(1, 2)).astype(BF16)
+        out[k, p.own(0), :] = (half[k % KEPT, p.rows(1, 0), :] + p.landed(1, 1) + p.landed(1, 2)).astype(BF16)
         p.reduce_copy(1, 0).wait_send()
         p.reduce_copy(1, 1).wait_send()
         p.gather(2, 0).start()
@@ -229,7 +234,7 @@
 
     @pl.loop(0, pieces + LAGS[-1])
     def _(i):
-        for s in reversed(range(len(stages))):
+        for s in ORDER:
             k = i - LAGS[s]
 
             @pl.when((k >= 0) & (k < pieces))
@@ -270,12 +275,12 @@
                 pltpu.VMEM((d, tokens), BF16),
                 pltpu.VMEM((d, tokens), BF16),
                 pltpu.VMEM((AHEAD + 1, tokens, WIDTH), BF16),
-                pltpu.VMEM((LEAVING, d, WIDTH), F32),
-                pltpu.VMEM((LEAVING, quarter, WIDTH), F32),
-                pltpu.VMEM((LEAVING, 3, quarter, WIDTH), BF16),
-                pltpu.VMEM((LEAVING, 3, part, WIDTH), BF16),
-                pltpu.VMEM((LANDING, 3, quarter, WIDTH), BF16),
-                pltpu.VMEM((LANDING, 3, part, WIDTH), BF16),
+                pltpu.VMEM((KEPT, d, WIDTH), F32),
+                pltpu.VMEM((KEPT, quarter, WIDTH), F32),
+                pltpu.VMEM((KEPT, 3, quarter, WIDTH), BF16),
+                pltpu.VMEM((KEPT, 3, part, WIDTH), BF16),
+                pltpu.VMEM((HELD, 3, quarter, WIDTH), BF16),
+                pltpu.VMEM((HELD, 3, part, WIDTH), BF16),
                 pltpu.SemaphoreType.DMA((RAW,)),
                 pltpu.SemaphoreType.DMA((AHEAD + 1,)),
                 pltpu.SemaphoreType.DMA((4, 3, LEAVING)),

time: 199 us -> 198 us (level)
  no operation moved by 1% of the time
where the time goes in v3:
time: 198 us
  Pallas kernels  198 us (100%)
    pallas_call x1, Pallas kernels, local(): pl.pallas_call(functools.partial(kernel, side), out_shape=pltpu.VMEM((pie...  192 us
    pallas_call x1, Pallas kernels, local(): pl.pallas_call(place, out_shape=jax.ShapeDtypeStruct((matrices, d, ff), B...  6.04 us

profile of v3, /device:TPU:97, one launch (start us, length us, event | category | flops | bytes accessed | tf_op | source)
XLA Modules:
  0.0 197.9 jit_solution(12518408911644456478)
XLA Ops:
  0.0 191.8 %sum_over_group.1.held = bf16[36,896,256]{2,1,0:T(8,128)(2,1)S(1)} custom-call(bf16[4,4096,896]{2,1,0:T(8,128)(2,1)} %bitcast.2, bf16[4,4096,2304]{2,1,0:T(8,128)(2,1)} %bitcast.1.g_hbm), custom_call_target="tpu_custom_call" | custom-call | flops 67645734912 | bytes 104857600 | tf_op jit(solution)/shard_map/sum_over_group/pallas_call | solution.py:268
  191.8 6.0 %place.1 = bf16[4,896,2304]{2,1,0:T(8,128)(2,1)} custom-call(bf16[36,896,256]{2,1,0:T(8,128)(2,1)S(1)} %sum_over_group.1.held), custom_call_target="tpu_custom_call" | custom-call | tf_op jit(solution)/shard_map/place/pallas_call | solution.py:299
